TPU v7x, 256 devices: a whole 4x4x8 slice. The times are simulated.
256 devices in a mesh: bins: 16 (over x, z_lo, core), sta: 16 (over z_hi, y).
Axes of the slice: x: 4, y: 4, z: 8 (z_hi: 4, z_lo: 2; z = z_hi * 2 + z_lo), core: 2. Of those that a mesh axis runs over, the one named last changes fastest.
Arguments:
- spectra: bfloat16 [2, 128, 8, 4096], P(None, 'bins', None, 'sta'), may hold values from -110 to 110
- coords: int32 [2, 4096], replicated, may hold values from 0 to 2047
- slowness: int32 [2, 2048], replicated, may hold values from -32 to 31
Outputs:
- beam_power: float32 [128, 2048], P('bins', 'sta')
All inputs are finite; a program needn't handle non-finite values.
Results may differ from a plain program's by a relative error of at most 0.002.
Values may be sent and summed in bfloat16 or wider, within the bound.
A program may use at most 64 MiB of HBM per device.

v0:
```python
import jax
import jax.numpy as jnp
import numpy as np
from jax import lax
from jax.experimental import pallas as pl
from jax.experimental.pallas import tpu as pltpu
from jax.sharding import PartitionSpec as P

MESH = pl.DeviceIdType.MESH
epsilon = 1e-06
scope = jax.named_scope

GROUPS = (
    ((0, 0), (0, 1), (0, 3), (0, 2)),
    ((1, 0), (3, 0), (1, 1), (3, 3)),
    ((1, 3), (3, 1), (1, 2), (3, 2)),
    ((2, 0), (2, 1), (2, 3), (2, 2)),
)
FAR = [(o, g) for g in range(3, -1, -1) for o in GROUPS[g][::-1]]
FAR_BINS = sorted(((dx, dl) for dx in range(4) for dl in range(2)), key=lambda o: -min(o[0], 4 - o[0]) - o[1])


def cheb_fit(fn, degree):
    nodes = np.cos(np.pi * (np.arange(4001) + 0.5) / 4001)
    u = (nodes + 1.0) / 2.0
    return np.polynomial.chebyshev.Chebyshev.fit(u, fn(u), degree, domain=[0, 1]).convert(
        kind=np.polynomial.Polynomial
    ).coef


COS = [float(c) for c in cheb_fit(lambda u: np.cos(np.pi * np.sqrt(u)), 7)]
SIN = [float(c) for c in cheb_fit(lambda u: np.pi * np.sinc(np.sqrt(u)), 6)]


def horner(coefs, u):
    acc = jnp.full_like(u, coefs[-1])
    for c in coefs[-2::-1]:
        acc = acc * u + c
    return acc


def cos_sin(index):
    t = lax.shift_right_arithmetic(lax.shift_left(index, 11), 11).astype(jnp.float32) * (1.0 / 1048576)
    u = t * t
    return horner(COS, u), horner(SIN, u) * t


def iota(shape, dim):
    return lax.broadcasted_iota(jnp.int32, shape, dim)


def kernel(
    x_hbm, co_hbm, sl_hbm, out_ref,
    xv, cov, slv, raw_send, raw_recv, part_send, part_recv, tot_send, tot_recv, pow_send, pow_recv,
    tabc, tabt, tabr, xrot, wbuf, accum,
    in_sem, part_ss, part_rs, raw_ss, raw_rs, tot_ss, tot_rs, pow_ss, pow_rs,
):
    bi = lax.axis_index("bins")
    sj = lax.axis_index("sta")
    core = lax.rem(bi, 2)
    chip = bi - core
    px = lax.div(bi, 4)
    pl_lo = lax.rem(lax.div(bi, 2), 2)
    pz = lax.div(sj, 4)
    py = lax.rem(sj, 4)
    pair = lax.div(sj, 8)
    own = lax.rem(sj, 8)
    f1 = bi * 8 + own + 1

    def sta_at(o):
        return lax.rem(pz + o[0], 4) * 4 + lax.rem(py + o[1], 4)

    def chip_at(o):
        return lax.rem(px + o[0], 4) * 4 + lax.rem(pl_lo + o[1], 2) * 2

    loads = [
        pltpu.make_async_copy(src, dst, in_sem.at[n])
        for n, (src, dst) in enumerate(((x_hbm, xv), (co_hbm, cov), (sl_hbm, slv)))
    ]
    for load in loads:
        load.start()

    barrier = pltpu.get_barrier_semaphore()

    def greet(b, s):
        pl.semaphore_signal(barrier, inc=1, device_id=(b, s), device_id_type=MESH)

    def loop(lo, hi, body):
        lax.fori_loop(lo, hi, lambda d, c: (body(d), c)[1], 0)

    with scope("a_greet"):
        @pl.when(core == 1)
        def _():
            for o in FAR_BINS:
                greet(chip_at(o), sj)
                if o != (0, 0):
                    greet(chip_at(o) + 1, sj)

        @pl.when(core == 0)
        def _():
            loop(0, 16, lambda d: greet(chip + 1, lax.rem(sj + d, 16)))

        loop(1, 16, lambda d: greet(bi, lax.rem(sj + d, 16)))

    with scope("b_xwait"):
        loads[0].wait()

    with scope("c_sumsq"):
        sq = jnp.zeros((8, 256), jnp.float32)
        for b in range(8):
            re = xv[0, b].astype(jnp.float32)
            im = xv[1, b].astype(jnp.float32)
            sq = sq + (re * re + im * im)
            raw_send[b] = jnp.concatenate(
                [re[:, :128], im[:, :128], re[:, 128:], im[:, 128:]], 0
            ).astype(jnp.bfloat16)
        part = jnp.concatenate([sq[:, :128], sq[:, 128:]], 0).astype(jnp.bfloat16)
        part_send[...] = part

    with scope("d_barrier"):
        @pl.when(core == 1)
        def _():
            pl.semaphore_wait(barrier, 38)

        @pl.when(core == 0)
        def _():
            pl.semaphore_wait(barrier, 23)

    def part_copy(n):
        return pltpu.make_async_remote_copy(
            src_ref=part_send, dst_ref=part_recv.at[bi],
            send_sem=part_ss, recv_sem=part_rs,
            device_id=(chip_at(FAR_BINS[n]) + 1, sj), device_id_type=MESH,
        )

    def raw_copy(n):
        q = sta_at(FAR[n][0])
        return pltpu.make_async_remote_copy(
            src_ref=raw_send.at[lax.rem(q, 8)], dst_ref=raw_recv.at[sj],
            send_sem=raw_ss, recv_sem=raw_rs,
            device_id=(bi, q), device_id_type=MESH,
        )

    def tot_copy(n, c):
        return pltpu.make_async_remote_copy(
            src_ref=tot_send, dst_ref=tot_recv.at[sj],
            send_sem=tot_ss.at[c], recv_sem=tot_rs.at[FAR[n][1]],
            device_id=(chip + c, sta_at(FAR[n][0])), device_id_type=MESH,
        )

    def pow_copy(d):
        m = lax.rem(own + d, 8)
        return pltpu.make_async_remote_copy(
            src_ref=pow_send.at[m], dst_ref=pow_recv.at[own],
            send_sem=pow_ss, recv_sem=pow_rs,
            device_id=(bi, pair * 8 + m), device_id_type=MESH,
        )

    def wait_all(buf, count, sem):
        blocks = buf.at[pl.ds(0, count)]
        pltpu.make_async_copy(blocks, blocks, sem).wait()

    with scope("e_send1"):
        for n in range(7):
            part_copy(n).start()

        @pl.when(core == 0)
        def _():
            part_copy(7).start()

        @pl.when(core == 1)
        def _():
            part_recv[bi] = part

        for n in range(15):
            raw_copy(n).start()
        raw_recv[sj] = raw_send[own]

    loads[1].wait()
    loads[2].wait()
    row8 = iota((8, 256), 0)
    odd32 = iota((32, 256), 0) * 2 + 1
    coarse = row8 * 8 + 4
    fine = jnp.where(row8 == 0, 1, 3)

    def tables(j):
        lanes = pl.ds(pl.multiple_of(j * 256, 256), 256)
        cx = cov[0:1, lanes] * f1
        cy = cov[1:2, lanes] * f1
        c, s = cos_sin(coarse * cx)
        tabc[0, :, lanes] = c
        tabc[1, :, lanes] = s
        c, s = cos_sin(jnp.where(row8 < 2, fine * cx, jnp.broadcast_to(cx + cy, (8, 256))))
        tabr[0, :, lanes] = c
        tabr[1, :, lanes] = s
        cyt, syt = cos_sin(odd32 * cy)
        cols = []
        for trig in range(2):
            for tab in (cyt, syt):
                for f in range(2):
                    cols.append(tabr[trig, f : f + 1, lanes] * tab)
        tabt[lanes, :] = jnp.concatenate(cols, 0).astype(jnp.bfloat16).T

    with scope("f_tables"):
        loop(0, 16, tables)

    @pl.when(core == 1)
    def _():
        with scope("g_partwait"):
            wait_all(part_recv, 15, part_rs)
        with scope("h_total"):
            total = part_recv[0].astype(jnp.float32)
            for p in range(1, 16):
                total = total + part_recv[p].astype(jnp.float32)
            total = total.astype(jnp.bfloat16)
            tot_send[...] = total
            for n in range(15):
                tot_copy(n, 0).start()
                tot_copy(n, 1).start()
            tot_copy(15, 0).start()
            tot_recv[sj] = total

    with scope("i_pick"):
        beams = pl.ds(pl.multiple_of(pair * 1024, 1024), 1024)
        sx = slv[0:1, beams]
        sy = slv[1:2, beams]
        u = sx + 32
        m = lax.shift_right_arithmetic(u, 2)
        f = u & 3
        cpos = m >= 8
        fpos = f >= 2
        ypos = sy >= 0
        cidx = jnp.where(cpos, m - 8, 7 - m)
        fidx = jnp.where(fpos, f - 2, 1 - f)
        ky = jnp.where(ypos, sy, -1 - sy)
        c01 = jnp.where(cpos, 1, 0)
        rel = jnp.where(c01 == jnp.where(fpos, 1, 0), 0, 1)
        diff = jnp.where(c01 == jnp.where(ypos, 1, 0), 0, 1)
        pick_row = (rel * 2 + diff) * 8 + cidx
        pick_col = (1 - c01) * 64 + fidx * 32 + ky
    with scope("j_rawwait"):
        wait_all(raw_recv, 15, raw_rs)

    def rotate(j):
        lanes = pl.ds(pl.multiple_of(j * 256, 256), 256)
        raw = raw_recv[j].astype(jnp.float32)
        re = jnp.concatenate([raw[:8], raw[16:24]], 1)
        im = jnp.concatenate([raw[8:16], raw[24:]], 1)
        c = tabr[0, 2:3, lanes]
        s = tabr[1, 2:3, lanes]
        xrot[0:8, lanes] = re * c - im * s
        xrot[8:16, lanes] = im * c + re * s

    with scope("k_rotate"):
        loop(0, 16, rotate)

    for group in range(4):
        with scope("l_totwait"):
            if group == 0:
                @pl.when(core == 0)
                def _():
                    wait_all(tot_recv, 4, tot_rs.at[group])

                @pl.when(core == 1)
                def _():
                    wait_all(tot_recv, 3, tot_rs.at[group])
            else:
                wait_all(tot_recv, 4, tot_rs.at[group])
        with scope("m_main"):
            acc = None
            for n in range(4 * group, 4 * group + 4):
                j = sta_at(GROUPS[group][n % 4])
                lanes = pl.ds(pl.multiple_of(j * 256, 256), 256)
                inv = lax.rsqrt(tot_recv[j].astype(jnp.float32) * (1.0 / 256) + epsilon)
                inv = jnp.concatenate([inv[:8], inv[8:]], 1)
                at = slice(n * 256, n * 256 + 256)
                wbuf[0:8, at] = xrot[0:8, lanes] * inv
                wbuf[8:16, at] = xrot[8:16, lanes] * inv
                rows = []
                for trig in range(2):
                    tab = tabc[trig, :, lanes]
                    for row in range(16):
                        rows.append(wbuf[row : row + 1, at] * tab)
                v = jnp.concatenate(rows, 0).astype(jnp.bfloat16)
                term = lax.dot_general(
                    v, tabt[lanes, :], (((1,), (0,)), ((), ())), preferred_element_type=jnp.float32
                )
                acc = term if acc is None else acc + term
            if group == 0:
                accum[...] = acc
            elif group < 3:
                accum[...] += acc
            else:
                acc = acc + accum[...]

    with scope("n_post"):
        mark = jnp.where(iota((128, 128), 1) < 64, -1.0, 1.0)
        cc, cs, sc, ss = acc[:128, :128], acc[:128, 128:], acc[128:, :128], acc[128:, 128:]
        grid = []

        def seg_sum(a):
            a = a * a
            total = a[:8]
            for g in range(1, 8):
                total = total + a[8 * g : 8 * g + 8]
            return total

        for x, y in ((cc - ss, sc + cs), (cc + ss, sc - cs)):
            y = pltpu.roll(y, 64, 1) * mark
            plus, minus = x + y, x - y
            turned = pltpu.roll(plus[64:], 64, 1)
            grid.append(seg_sum(plus[:64] + turned) + pltpu.roll(seg_sum(plus[:64] - turned), 64, 1))
            turned = pltpu.roll(minus[64:], 64, 1)
            grid.append(seg_sum(minus[:64] - turned) + pltpu.roll(seg_sum(minus[:64] + turned), 64, 1))
        grid = jnp.concatenate(grid, 0) * (1.0 / 32768)
        row = iota((8, 128), 0)
        for n in range(8):
            at = slice(128 * n, 128 * n + 128)
            col = jnp.broadcast_to(pick_col[:, at], (8, 128))
            hit = jnp.broadcast_to(pick_row[:, at], (8, 128))
            total = jnp.zeros((8, 128), jnp.float32)
            for k in range(4):
                values = jnp.take_along_axis(grid[8 * k : 8 * k + 8], col, axis=1)
                total = total + jnp.where(row + 8 * k == hit, values, 0.0)
            pow_send[n] = jnp.sum(total, 0, keepdims=True)
    with scope("o_powsend"):
        for d in range(7, 0, -1):
            pow_copy(d).start()
        pow_recv[own] = pow_send[own]

    with scope("p_sendwait"):
        @pl.when(core == 0)
        def _():
            wait_all(part_recv, 8, part_ss)

        @pl.when(core == 1)
        def _():
            wait_all(part_recv, 7, part_ss)
            wait_all(tot_recv, 16, tot_ss.at[0])
            wait_all(tot_recv, 15, tot_ss.at[1])

        wait_all(raw_recv, 15, raw_ss)

    with scope("q_powwait"):
        wait_all(pow_recv, 7, pow_rs)

    with scope("r_end"):
        for b in range(8):
            out_ref[b : b + 1, :] = pow_recv[b]
        wait_all(pow_recv, 7, pow_ss)


def local(spectra, coords, slowness):
    f32, bf16, i32 = jnp.float32, jnp.bfloat16, jnp.int32
    dma = pltpu.SemaphoreType.DMA
    return pl.pallas_call(
        kernel,
        out_shape=jax.ShapeDtypeStruct((8, 128), f32),
        in_specs=[pl.BlockSpec(memory_space=pl.ANY)] * 3,
        out_specs=pl.BlockSpec(memory_space=pltpu.VMEM),
        scratch_shapes=[
            pltpu.VMEM((2, 8, 8, 256), bf16),
            pltpu.VMEM((2, 4096), i32),
            pltpu.VMEM((2, 2048), i32),
            pltpu.VMEM((8, 32, 128), bf16),
            pltpu.VMEM((16, 32, 128), bf16),
            pltpu.VMEM((16, 128), bf16),
            pltpu.VMEM((16, 16, 128), bf16),
            pltpu.VMEM((16, 128), bf16),
            pltpu.VMEM((16, 16, 128), bf16),
            pltpu.VMEM((8, 1, 128), f32),
            pltpu.VMEM((8, 1, 128), f32),
            pltpu.VMEM((2, 8, 4096), f32),
            pltpu.VMEM((4096, 256), bf16),
            pltpu.VMEM((2, 8, 4096), f32),
            pltpu.VMEM((16, 4096), f32),
            pltpu.VMEM((16, 4096), f32),
            pltpu.VMEM((256, 256), f32),
            dma((3,)),
            dma, dma, dma, dma, dma((2,)), dma((4,)), dma, dma,
        ],
        compiler_params=pltpu.CompilerParams(
            collective_id=0, has_side_effects=True, vmem_limit_bytes=56540000
        ),
    )(spectra, coords, slowness)


def solution(mesh):
    in_specs = (P(None, "bins", None, "sta"), P(), P())
    out_specs = P("bins", "sta")
    return jax.shard_map(local, mesh=mesh, in_specs=in_specs, out_specs=out_specs, check_vma=False)
```

profile of v0, /device:TPU:1, one launch (start us, length us, event | category | flops | bytes accessed | tf_op | source)
XLA Modules:
  0.0 26.0 jit_solution(6197553952568152858)
XLA Ops:
  0.0 25.4 %shard_map.37 = f32[8,128]{1,0:T(8,128)S(1)} custom-call(bf16[2,8,8,256]{3,2,1,0:T(8,128)(2,1)} %x_hbm.1, s32[2,4096]{1,0:T(2,128)} %co_hbm.1, s32[2,2048]{1,0:T(2,128)} %sl_hbm.1), custom_call_target="tpu_custom_call" | custom-call | tf_op jit(solution)/shard_map/pallas_call | solution.py:356
  25.4 0.6 %copy.5 = f32[8,128]{1,0:T(8,128)} copy(f32[8,128]{1,0:T(8,128)S(1)} %shard_map.37) | data formatting | bytes 8192
where the time goes:
time: 26.2 us; the launch traced here: 26 us
  Pallas kernels  25.4 us (97%)
  local copies, waits for them, and re-layouts  0.6 us (2%)
    pallas_call x1, Pallas kernels, local(): pl.pallas_call(kernel, out_shape=jax.ShapeDtypeStruct((8, 128), f32), in_...  25.4 us
    unnamed x1, local copies, waits for them, and re-layouts  0.6 us

commit v1 on v0

--- a/solution.py
+++ b/solution.py
@@ -10,13 +10,7 @@
 epsilon = 1e-06
 scope = jax.named_scope
 
-GROUPS = (
-    ((0, 0), (0, 1), (0, 3), (0, 2)),
-    ((1, 0), (3, 0), (1, 1), (3, 3)),
-    ((1, 3), (3, 1), (1, 2), (3, 2)),
-    ((2, 0), (2, 1), (2, 3), (2, 2)),
-)
-FAR = [(o, g) for g in range(3, -1, -1) for o in GROUPS[g][::-1]]
+FAR_Y = (2, 1, 3, 0)
 FAR_BINS = sorted(((dx, dl) for dx in range(4) for dl in range(2)), key=lambda o: -min(o[0], 4 - o[0]) - o[1])
 
 
@@ -53,7 +47,7 @@
     x_hbm, co_hbm, sl_hbm, out_ref,
     xv, cov, slv, raw_send, raw_recv, part_send, part_recv, tot_send, tot_recv, pow_send, pow_recv,
     tabc, tabt, tabr, xrot, wbuf, accum,
-    in_sem, part_ss, part_rs, raw_ss, raw_rs, tot_ss, tot_rs, pow_ss, pow_rs,
+    in_sem, late_sem, part_ss, part_rs, raw_ss, raw_rs, tot_ss, tot_rs, pow_ss, pow_rs,
 ):
     bi = lax.axis_index("bins")
     sj = lax.axis_index("sta")
@@ -67,8 +61,12 @@
     own = lax.rem(sj, 8)
     f1 = bi * 8 + own + 1
 
-    def sta_at(o):
-        return lax.rem(pz + o[0], 4) * 4 + lax.rem(py + o[1], 4)
+    early = pz < 2
+    late = pz >= 2
+    rows = (pz, pz + 1 - 2 * lax.rem(pz, 2), 3 - pz, lax.rem(pz + 2, 4))
+
+    def sta_at(n, dy):
+        return rows[n] * 4 + lax.rem(py + dy, 4)
 
     def chip_at(o):
         return lax.rem(px + o[0], 4) * 4 + lax.rem(pl_lo + o[1], 2) * 2
@@ -88,6 +86,18 @@
     def loop(lo, hi, body):
         lax.fori_loop(lo, hi, lambda d, c: (body(d), c)[1], 0)
 
+    def greet_rows(b, first, last):
+        loop(first * 4, last * 4, lambda q: greet(b, q))
+
+    def greet_peers(first, last):
+        @pl.when((pz >= first) & (pz < last))
+        def _():
+            loop(1, 4 * (last - first), lambda d: greet(bi, first * 4 + lax.rem(sj - first * 4 + d, 4 * (last - first))))
+
+        @pl.when((pz < first) | (pz >= last))
+        def _():
+            greet_rows(bi, first, last)
+
     with scope("a_greet"):
         @pl.when(core == 1)
         def _():
@@ -96,11 +106,23 @@
                 if o != (0, 0):
                     greet(chip_at(o) + 1, sj)
 
+            @pl.when(early)
+            def _():
+                greet_rows(chip, 2, 4)
+
         @pl.when(core == 0)
         def _():
-            loop(0, 16, lambda d: greet(chip + 1, lax.rem(sj + d, 16)))
-
-        loop(1, 16, lambda d: greet(bi, lax.rem(sj + d, 16)))
+            greet_rows(chip + 1, 2, 4)
+
+            @pl.when(early)
+            def _():
+                greet_rows(chip + 1, 0, 2)
+
+        greet_peers(2, 4)
+
+        @pl.when(early)
+        def _():
+            greet_peers(0, 2)
 
     with scope("b_xwait"):
         loads[0].wait()
@@ -118,13 +140,12 @@
         part_send[...] = part
 
     with scope("d_barrier"):
-        @pl.when(core == 1)
-        def _():
-            pl.semaphore_wait(barrier, 38)
-
-        @pl.when(core == 0)
-        def _():
-            pl.semaphore_wait(barrier, 23)
+        for cond, count in (
+            (early & (core == 1), 22), (late & (core == 1), 38), (early & (core == 0), 15), (late & (core == 0), 31)
+        ):
+            @pl.when(cond)
+            def _(count=count):
+                pl.semaphore_wait(barrier, count)
 
     def part_copy(n):
         return pltpu.make_async_remote_copy(
@@ -133,20 +154,31 @@
             device_id=(chip_at(FAR_BINS[n]) + 1, sj), device_id_type=MESH,
         )
 
-    def raw_copy(n):
-        q = sta_at(FAR[n][0])
+    def raw_copy(n, dy):
+        q = sta_at(n, dy)
         return pltpu.make_async_remote_copy(
             src_ref=raw_send.at[lax.rem(q, 8)], dst_ref=raw_recv.at[sj],
-            send_sem=raw_ss, recv_sem=raw_rs,
+            send_sem=raw_ss, recv_sem=raw_rs.at[n // 2],
             device_id=(bi, q), device_id_type=MESH,
         )
 
-    def tot_copy(n, c):
+    def tot_copy(n, dy, c):
         return pltpu.make_async_remote_copy(
             src_ref=tot_send, dst_ref=tot_recv.at[sj],
-            send_sem=tot_ss.at[c], recv_sem=tot_rs.at[FAR[n][1]],
-            device_id=(chip + c, sta_at(FAR[n][0])), device_id_type=MESH,
+            send_sem=tot_ss.at[c], recv_sem=tot_rs.at[n],
+            device_id=(chip + c, sta_at(n, dy)), device_id_type=MESH,
         )
+
+    def send_raw(n):
+        for dy in FAR_Y:
+            if (n, dy) != (0, 0):
+                raw_copy(n, dy).start()
+
+    def send_tot(n):
+        for dy in FAR_Y:
+            tot_copy(n, dy, 0).start()
+            if (n, dy) != (0, 0):
+                tot_copy(n, dy, 1).start()
 
     def pow_copy(d):
         m = lax.rem(own + d, 8)
@@ -172,8 +204,22 @@
         def _():
             part_recv[bi] = part
 
-        for n in range(15):
-            raw_copy(n).start()
+        @pl.when(late)
+        def _():
+            def announce(b):
+                loop(0, 8, lambda q: pl.semaphore_signal(late_sem, inc=1, device_id=(b, q), device_id_type=MESH))
+
+            announce(bi)
+
+            @pl.when(core == 0)
+            def _():
+                announce(chip + 1)
+
+            send_raw(3)
+            send_raw(2)
+
+        send_raw(1)
+        send_raw(0)
         raw_recv[sj] = raw_send[own]
 
     loads[1].wait()
@@ -214,10 +260,14 @@
                 total = total + part_recv[p].astype(jnp.float32)
             total = total.astype(jnp.bfloat16)
             tot_send[...] = total
-            for n in range(15):
-                tot_copy(n, 0).start()
-                tot_copy(n, 1).start()
-            tot_copy(15, 0).start()
+
+            @pl.when(late)
+            def _():
+                send_tot(3)
+                send_tot(2)
+
+            send_tot(1)
+            send_tot(0)
             tot_recv[sj] = total
 
     with scope("i_pick"):
@@ -238,57 +288,75 @@
         diff = jnp.where(c01 == jnp.where(ypos, 1, 0), 0, 1)
         pick_row = (rel * 2 + diff) * 8 + cidx
         pick_col = (1 - c01) * 64 + fidx * 32 + ky
-    with scope("j_rawwait"):
-        wait_all(raw_recv, 15, raw_rs)
-
-    def rotate(j):
-        lanes = pl.ds(pl.multiple_of(j * 256, 256), 256)
-        raw = raw_recv[j].astype(jnp.float32)
-        re = jnp.concatenate([raw[:8], raw[16:24]], 1)
-        im = jnp.concatenate([raw[8:16], raw[24:]], 1)
-        c = tabr[0, 2:3, lanes]
-        s = tabr[1, 2:3, lanes]
-        xrot[0:8, lanes] = re * c - im * s
-        xrot[8:16, lanes] = im * c + re * s
-
-    with scope("k_rotate"):
-        loop(0, 16, rotate)
-
-    for group in range(4):
-        with scope("l_totwait"):
-            if group == 0:
+    with scope("i_late"):
+        @pl.when(early & (core == 1))
+        def _():
+            pl.semaphore_wait(late_sem, 16)
+            send_tot(2)
+            send_tot(3)
+
+        @pl.when(early & (core == 0))
+        def _():
+            pl.semaphore_wait(late_sem, 8)
+
+        @pl.when(early)
+        def _():
+            send_raw(2)
+            send_raw(3)
+
+    def rotate(n):
+        def block(y):
+            j = rows[n] * 4 + y
+            lanes = pl.ds(pl.multiple_of(j * 256, 256), 256)
+            raw = raw_recv[j].astype(jnp.float32)
+            re = jnp.concatenate([raw[:8], raw[16:24]], 1)
+            im = jnp.concatenate([raw[8:16], raw[24:]], 1)
+            c = tabr[0, 2:3, lanes]
+            s = tabr[1, 2:3, lanes]
+            xrot[0:8, lanes] = re * c - im * s
+            xrot[8:16, lanes] = im * c + re * s
+
+        loop(0, 4, block)
+
+    for n in range(4):
+        if n % 2 == 0:
+            with scope("j_rawwait"):
+                wait_all(raw_recv, 7 + n // 2, raw_rs.at[n // 2])
+            with scope("k_rotate"):
+                rotate(n)
+                rotate(n + 1)
+        with scope("l_totwait%d" % n):
+            if n == 0:
                 @pl.when(core == 0)
                 def _():
-                    wait_all(tot_recv, 4, tot_rs.at[group])
+                    wait_all(tot_recv, 4, tot_rs.at[0])
 
                 @pl.when(core == 1)
                 def _():
-                    wait_all(tot_recv, 3, tot_rs.at[group])
+                    wait_all(tot_recv, 3, tot_rs.at[0])
             else:
-                wait_all(tot_recv, 4, tot_rs.at[group])
+                wait_all(tot_recv, 4, tot_rs.at[n])
         with scope("m_main"):
-            acc = None
-            for n in range(4 * group, 4 * group + 4):
-                j = sta_at(GROUPS[group][n % 4])
-                lanes = pl.ds(pl.multiple_of(j * 256, 256), 256)
-                inv = lax.rsqrt(tot_recv[j].astype(jnp.float32) * (1.0 / 256) + epsilon)
-                inv = jnp.concatenate([inv[:8], inv[8:]], 1)
-                at = slice(n * 256, n * 256 + 256)
-                wbuf[0:8, at] = xrot[0:8, lanes] * inv
-                wbuf[8:16, at] = xrot[8:16, lanes] * inv
-                rows = []
-                for trig in range(2):
-                    tab = tabc[trig, :, lanes]
-                    for row in range(16):
-                        rows.append(wbuf[row : row + 1, at] * tab)
-                v = jnp.concatenate(rows, 0).astype(jnp.bfloat16)
-                term = lax.dot_general(
-                    v, tabt[lanes, :], (((1,), (0,)), ((), ())), preferred_element_type=jnp.float32
-                )
-                acc = term if acc is None else acc + term
-            if group == 0:
+            lanes = pl.ds(pl.multiple_of(rows[n] * 1024, 1024), 1024)
+            at = slice(n * 1024, n * 1024 + 1024)
+            parts = []
+            for y in range(4):
+                total = tot_recv[rows[n] * 4 + y].astype(jnp.float32)
+                parts += [total[:8], total[8:]]
+            inv = lax.rsqrt(jnp.concatenate(parts, 1) * (1.0 / 256) + epsilon)
+            wbuf[0:8, at] = xrot[0:8, lanes] * inv
+            wbuf[8:16, at] = xrot[8:16, lanes] * inv
+            v = []
+            for trig in range(2):
+                tab = tabc[trig, :, lanes]
+                for row in range(16):
+                    v.append(wbuf[row : row + 1, at] * tab)
+            acc = jnp.dot(
+                jnp.concatenate(v, 0).astype(jnp.bfloat16), tabt[lanes, :], preferred_element_type=jnp.float32
+            )
+            if n == 0:
                 accum[...] = acc
-            elif group < 3:
+            elif n < 3:
                 accum[...] += acc
             else:
                 acc = acc + accum[...]
@@ -377,7 +445,8 @@
             pltpu.VMEM((16, 4096), f32),
             pltpu.VMEM((256, 256), f32),
             dma((3,)),
-            dma, dma, dma, dma, dma((2,)), dma((4,)), dma, dma,
+            pltpu.SemaphoreType.REGULAR,
+            dma, dma, dma, dma((2,)), dma((2,)), dma((4,)), dma, dma,
         ],
         compiler_params=pltpu.CompilerParams(
             collective_id=0, has_side_effects=True, vmem_limit_bytes=56540000

time: 26.2 us -> 24.9 us (0.950)
  Pallas kernels: 25.4 us -> 24.2 us
    pallas_call x1, Pallas kernels: 25.4 us -> 24.2 us  [local(): pl.pallas_call(kernel, out_shape=jax.ShapeDtypeStruct((8, 128), f32), in_...]
where the time goes in v1:
time: 24.9 us; the launch traced here: 24.8 us
  Pallas kernels  24.2 us (97%)
  local copies, waits for them, and re-layouts  0.6 us (2%)
    pallas_call x1, Pallas kernels, local(): pl.pallas_call(kernel, out_shape=jax.ShapeDtypeStruct((8, 128), f32), in_...  24.2 us
    unnamed x1, local copies, waits for them, and re-layouts  0.6 us

profile of v1, /device:TPU:1, one launch (start us, length us, event | category | flops | bytes accessed | tf_op | source)
XLA Modules:
  0.0 24.8 jit_solution(7904298205579612780)
XLA Ops:
  0.0 24.2 %shard_map.37 = f32[8,128]{1,0:T(8,128)S(1)} custom-call(bf16[2,8,8,256]{3,2,1,0:T(8,128)(2,1)} %x_hbm.1, s32[2,4096]{1,0:T(2,128)} %co_hbm.1, s32[2,2048]{1,0:T(2,128)} %sl_hbm.1), custom_call_target="tpu_custom_call" | custom-call | tf_op jit(solution)/shard_map/pallas_call | solution.py:424
  24.2 0.6 %copy.5 = f32[8,128]{1,0:T(8,128)} copy(f32[8,128]{1,0:T(8,128)S(1)} %shard_map.37) | data formatting | bytes 8192

commit v2 on v1

--- a/solution.py
+++ b/solution.py
@@ -45,9 +45,9 @@
 
 def kernel(
     x_hbm, co_hbm, sl_hbm, out_ref,
-    xv, cov, slv, raw_send, raw_recv, part_send, part_recv, tot_send, tot_recv, pow_send, pow_recv,
+    xv, cov, slv, raw_send, raw_recv, side_send, side_recv, part_send, part_recv, tot_send, tot_recv, pow_send, pow_recv,
     tabc, tabt, tabr, xrot, wbuf, accum,
-    in_sem, late_sem, part_ss, part_rs, raw_ss, raw_rs, tot_ss, tot_rs, pow_ss, pow_rs,
+    in_sem, late_sem, go_sem, side_ss, side_rs, part_ss, part_rs, raw_ss, raw_rs, tot_ss, tot_rs, pow_ss, pow_rs,
 ):
     bi = lax.axis_index("bins")
     sj = lax.axis_index("sta")
@@ -86,43 +86,24 @@
     def loop(lo, hi, body):
         lax.fori_loop(lo, hi, lambda d, c: (body(d), c)[1], 0)
 
-    def greet_rows(b, first, last):
-        loop(first * 4, last * 4, lambda q: greet(b, q))
-
-    def greet_peers(first, last):
-        @pl.when((pz >= first) & (pz < last))
-        def _():
-            loop(1, 4 * (last - first), lambda d: greet(bi, first * 4 + lax.rem(sj - first * 4 + d, 4 * (last - first))))
-
-        @pl.when((pz < first) | (pz >= last))
-        def _():
-            greet_rows(bi, first, last)
-
     with scope("a_greet"):
         @pl.when(core == 1)
         def _():
-            for o in FAR_BINS:
-                greet(chip_at(o), sj)
-                if o != (0, 0):
-                    greet(chip_at(o) + 1, sj)
+            greet(chip, sj)
+            for o in FAR_BINS[:7]:
+                greet(chip_at(o) + 1, sj)
 
             @pl.when(early)
             def _():
-                greet_rows(chip, 2, 4)
-
-        @pl.when(core == 0)
-        def _():
-            greet_rows(chip + 1, 2, 4)
-
-            @pl.when(early)
+                loop(1, 16, lambda d: greet(bi, lax.rem(sj + d, 16)))
+
+            @pl.when(late)
             def _():
-                greet_rows(chip + 1, 0, 2)
-
-        greet_peers(2, 4)
-
-        @pl.when(early)
-        def _():
-            greet_peers(0, 2)
+                loop(1, 8, lambda d: greet(bi, 8 + lax.rem(sj + d, 8)))
+
+        @pl.when(early & (core == 0))
+        def _():
+            loop(1, 16, lambda d: greet(chip + 1, lax.rem(sj + d, 16)))
 
     with scope("b_xwait"):
         loads[0].wait()
@@ -136,20 +117,20 @@
             raw_send[b] = jnp.concatenate(
                 [re[:, :128], im[:, :128], re[:, 128:], im[:, 128:]], 0
             ).astype(jnp.bfloat16)
-        part = jnp.concatenate([sq[:, :128], sq[:, 128:]], 0).astype(jnp.bfloat16)
-        part_send[...] = part
-
-    with scope("d_barrier"):
-        for cond, count in (
-            (early & (core == 1), 22), (late & (core == 1), 38), (early & (core == 0), 15), (late & (core == 0), 31)
-        ):
-            @pl.when(cond)
-            def _(count=count):
-                pl.semaphore_wait(barrier, count)
+        side = jnp.concatenate([sq[:, :128], sq[:, 128:]], 0)
+        side_send[...] = side
+
+    side_copy = pltpu.make_async_remote_copy(
+        src_ref=side_send, dst_ref=side_recv, send_sem=side_ss, recv_sem=side_rs,
+        device_id=(chip + 1, sj), device_id_type=MESH,
+    )
+
+    def go(n):
+        pl.semaphore_signal(go_sem.at[n], inc=1, device_id=(chip, sj), device_id_type=MESH)
 
     def part_copy(n):
         return pltpu.make_async_remote_copy(
-            src_ref=part_send, dst_ref=part_recv.at[bi],
+            src_ref=part_send, dst_ref=part_recv.at[lax.div(bi, 2)],
             send_sem=part_ss, recv_sem=part_rs,
             device_id=(chip_at(FAR_BINS[n]) + 1, sj), device_id_type=MESH,
         )
@@ -192,34 +173,58 @@
         blocks = buf.at[pl.ds(0, count)]
         pltpu.make_async_copy(blocks, blocks, sem).wait()
 
+    with scope("d_barrier"):
+        @pl.when(early & (core == 1))
+        def _():
+            pl.semaphore_wait(barrier, 21)
+
+        @pl.when(late & (core == 1))
+        def _():
+            pl.semaphore_wait(barrier, 30)
+
+        @pl.when(core == 0)
+        def _():
+            pl.semaphore_wait(barrier, 1)
+            side_copy.start()
+
+    with scope("e_side"):
+        @pl.when(core == 1)
+        def _():
+            side_copy.wait_recv()
+            part = (side + side_recv[...]).astype(jnp.bfloat16)
+            part_send[...] = part
+            for n in range(7):
+                part_copy(n).start()
+            go(0)
+            part_recv[lax.div(bi, 2)] = part
+
+            def announce(first, last):
+                def one(q):
+                    @pl.when(q != sj)
+                    def _():
+                        pl.semaphore_signal(late_sem, inc=1, device_id=(bi, q), device_id_type=MESH)
+
+                loop(first, last, one)
+
+            @pl.when(late)
+            def _():
+                announce(0, 16)
+
+        @pl.when(core == 0)
+        def _():
+            pl.semaphore_wait(go_sem.at[0], 1)
+
     with scope("e_send1"):
-        for n in range(7):
-            part_copy(n).start()
-
-        @pl.when(core == 0)
-        def _():
-            part_copy(7).start()
-
-        @pl.when(core == 1)
-        def _():
-            part_recv[bi] = part
-
         @pl.when(late)
         def _():
-            def announce(b):
-                loop(0, 8, lambda q: pl.semaphore_signal(late_sem, inc=1, device_id=(b, q), device_id_type=MESH))
-
-            announce(bi)
-
-            @pl.when(core == 0)
-            def _():
-                announce(chip + 1)
-
             send_raw(3)
             send_raw(2)
 
-        send_raw(1)
-        send_raw(0)
+        @pl.when(early)
+        def _():
+            send_raw(1)
+            send_raw(0)
+
         raw_recv[sj] = raw_send[own]
 
     loads[1].wait()
@@ -253,10 +258,10 @@
     @pl.when(core == 1)
     def _():
         with scope("g_partwait"):
-            wait_all(part_recv, 15, part_rs)
+            wait_all(part_recv, 7, part_rs)
         with scope("h_total"):
             total = part_recv[0].astype(jnp.float32)
-            for p in range(1, 16):
+            for p in range(1, 8):
                 total = total + part_recv[p].astype(jnp.float32)
             total = total.astype(jnp.bfloat16)
             tot_send[...] = total
@@ -266,8 +271,11 @@
                 send_tot(3)
                 send_tot(2)
 
-            send_tot(1)
-            send_tot(0)
+            @pl.when(early)
+            def _():
+                send_tot(1)
+                send_tot(0)
+
             tot_recv[sj] = total
 
     with scope("i_pick"):
@@ -291,18 +299,31 @@
     with scope("i_late"):
         @pl.when(early & (core == 1))
         def _():
-            pl.semaphore_wait(late_sem, 16)
+            pl.semaphore_wait(late_sem, 8)
+            go(1)
             send_tot(2)
             send_tot(3)
 
-        @pl.when(early & (core == 0))
-        def _():
-            pl.semaphore_wait(late_sem, 8)
+        @pl.when(late & (core == 1))
+        def _():
+            pl.semaphore_wait(late_sem, 7)
+            go(1)
+            send_tot(1)
+            send_tot(0)
+
+        @pl.when(core == 0)
+        def _():
+            pl.semaphore_wait(go_sem.at[1], 1)
 
         @pl.when(early)
         def _():
             send_raw(2)
             send_raw(3)
+
+        @pl.when(late)
+        def _():
+            send_raw(1)
+            send_raw(0)
 
     def rotate(n):
         def block(y):
@@ -399,7 +420,7 @@
     with scope("p_sendwait"):
         @pl.when(core == 0)
         def _():
-            wait_all(part_recv, 8, part_ss)
+            side_copy.wait_send()
 
         @pl.when(core == 1)
         def _():
@@ -432,8 +453,10 @@
             pltpu.VMEM((2, 2048), i32),
             pltpu.VMEM((8, 32, 128), bf16),
             pltpu.VMEM((16, 32, 128), bf16),
+            pltpu.VMEM((16, 128), f32),
+            pltpu.VMEM((16, 128), f32),
             pltpu.VMEM((16, 128), bf16),
-            pltpu.VMEM((16, 16, 128), bf16),
+            pltpu.VMEM((8, 16, 128), bf16),
             pltpu.VMEM((16, 128), bf16),
             pltpu.VMEM((16, 16, 128), bf16),
             pltpu.VMEM((8, 1, 128), f32),
@@ -446,6 +469,8 @@
             pltpu.VMEM((256, 256), f32),
             dma((3,)),
             pltpu.SemaphoreType.REGULAR,
+            pltpu.SemaphoreType.REGULAR((2,)),
+            dma, dma,
             dma, dma, dma, dma((2,)), dma((2,)), dma((4,)), dma, dma,
         ],
         compiler_params=pltpu.CompilerParams(

time: 24.9 us -> 24.5 us (0.984)
  Pallas kernels: 24.2 us -> 23.8 us
    pallas_call x1, Pallas kernels: 24.2 us -> 23.8 us  [local(): pl.pallas_call(kernel, out_shape=jax.ShapeDtypeStruct((8, 128), f32), in_...]
where the time goes in v2:
time: 24.5 us; the launch traced here: 24.4 us
  Pallas kernels  23.8 us (97%)
  local copies, waits for them, and re-layouts  0.6 us (2%)
    pallas_call x1, Pallas kernels, local(): pl.pallas_call(kernel, out_shape=jax.ShapeDtypeStruct((8, 128), f32), in_...  23.8 us
    unnamed x1, local copies, waits for them, and re-layouts  0.6 us

profile of v2, /device:TPU:1, one launch (start us, length us, event | category | flops | bytes accessed | tf_op | source)
XLA Modules:
  0.0 24.4 jit_solution(10509231143111178730)
XLA Ops:
  0.0 23.8 %shard_map.37 = f32[8,128]{1,0:T(8,128)S(1)} custom-call(bf16[2,8,8,256]{3,2,1,0:T(8,128)(2,1)} %x_hbm.1, s32[2,4096]{1,0:T(2,128)} %co_hbm.1, s32[2,2048]{1,0:T(2,128)} %sl_hbm.1), custom_call_target="tpu_custom_call" | custom-call | tf_op jit(solution)/shard_map/pallas_call | solution.py:445
  23.8 0.6 %copy.5 = f32[8,128]{1,0:T(8,128)} copy(f32[8,128]{1,0:T(8,128)S(1)} %shard_map.37) | data formatting | bytes 8192

commit v3 on v2

--- a/solution.py
+++ b/solution.py
@@ -47,7 +47,7 @@
     x_hbm, co_hbm, sl_hbm, out_ref,
     xv, cov, slv, raw_send, raw_recv, side_send, side_recv, part_send, part_recv, tot_send, tot_recv, pow_send, pow_recv,
     tabc, tabt, tabr, xrot, wbuf, accum,
-    in_sem, late_sem, go_sem, side_ss, side_rs, part_ss, part_rs, raw_ss, raw_rs, tot_ss, tot_rs, pow_ss, pow_rs,
+    in_sem, late_sem, go_sem, side_ss, side_rs, part_ss, part_rs, raw_ss, raw_rs, tot_ss, tot_rs, forward_ss, pow_ss, pow_rs,
 ):
     bi = lax.axis_index("bins")
     sj = lax.axis_index("sta")
@@ -143,11 +143,18 @@
             device_id=(bi, q), device_id_type=MESH,
         )
 
-    def tot_copy(n, dy, c):
+    def tot_copy(n, dy):
         return pltpu.make_async_remote_copy(
             src_ref=tot_send, dst_ref=tot_recv.at[sj],
-            send_sem=tot_ss.at[c], recv_sem=tot_rs.at[n],
-            device_id=(chip + c, sta_at(n, dy)), device_id_type=MESH,
+            send_sem=tot_ss, recv_sem=tot_rs.at[n],
+            device_id=(bi, sta_at(n, dy)), device_id_type=MESH,
+        )
+
+    def forward_copy(n):
+        block = tot_recv.at[pl.ds(rows[n] * 4, 4)]
+        return pltpu.make_async_remote_copy(
+            src_ref=block, dst_ref=block, send_sem=forward_ss, recv_sem=tot_rs.at[n],
+            device_id=(chip, sj), device_id_type=MESH,
         )
 
     def send_raw(n):
@@ -157,9 +164,8 @@
 
     def send_tot(n):
         for dy in FAR_Y:
-            tot_copy(n, dy, 0).start()
             if (n, dy) != (0, 0):
-                tot_copy(n, dy, 1).start()
+                tot_copy(n, dy).start()
 
     def pow_copy(d):
         m = lax.rem(own + d, 8)
@@ -347,16 +353,14 @@
                 rotate(n)
                 rotate(n + 1)
         with scope("l_totwait%d" % n):
-            if n == 0:
-                @pl.when(core == 0)
-                def _():
-                    wait_all(tot_recv, 4, tot_rs.at[0])
-
-                @pl.when(core == 1)
-                def _():
-                    wait_all(tot_recv, 3, tot_rs.at[0])
-            else:
+            @pl.when(core == 0)
+            def _(n=n):
                 wait_all(tot_recv, 4, tot_rs.at[n])
+
+            @pl.when(core == 1)
+            def _(n=n):
+                wait_all(tot_recv, 4 if n else 3, tot_rs.at[n])
+                forward_copy(n).start()
         with scope("m_main"):
             lanes = pl.ds(pl.multiple_of(rows[n] * 1024, 1024), 1024)
             at = slice(n * 1024, n * 1024 + 1024)
@@ -425,8 +429,8 @@
         @pl.when(core == 1)
         def _():
             wait_all(part_recv, 7, part_ss)
-            wait_all(tot_recv, 16, tot_ss.at[0])
-            wait_all(tot_recv, 15, tot_ss.at[1])
+            wait_all(tot_recv, 15, tot_ss)
+            wait_all(tot_recv, 16, forward_ss)
 
         wait_all(raw_recv, 15, raw_ss)
 
@@ -471,7 +475,7 @@
             pltpu.SemaphoreType.REGULAR,
             pltpu.SemaphoreType.REGULAR((2,)),
             dma, dma,
-            dma, dma, dma, dma((2,)), dma((2,)), dma((4,)), dma, dma,
+            dma, dma, dma, dma((2,)), dma, dma((4,)), dma, dma, dma,
         ],
         compiler_params=pltpu.CompilerParams(
             collective_id=0, has_side_effects=True, vmem_limit_bytes=56540000

time: 24.5 us -> 24 us (0.980)
  Pallas kernels: 23.8 us -> 23.3 us
    pallas_call x1, Pallas kernels: 23.8 us -> 23.3 us  [local(): pl.pallas_call(kernel, out_shape=jax.ShapeDtypeStruct((8, 128), f32), in_...]
where the time goes in v3:
time: 24 us; the launch traced here: 23.9 us
  Pallas kernels  23.3 us (97%)
  local copies, waits for them, and re-layouts  0.6 us (2%)
    pallas_call x1, Pallas kernels, local(): pl.pallas_call(kernel, out_shape=jax.ShapeDtypeStruct((8, 128), f32), in_...  23.3 us
    unnamed x1, local copies, waits for them, and re-layouts  0.6 us

profile of v3, /device:TPU:1, one launch (start us, length us, event | category | flops | bytes accessed | tf_op | source)
XLA Modules:
  0.0 23.9 jit_solution(18152077704773285208)
XLA Ops:
  0.0 23.3 %shard_map.37 = f32[8,128]{1,0:T(8,128)S(1)} custom-call(bf16[2,8,8,256]{3,2,1,0:T(8,128)(2,1)} %x_hbm.1, s32[2,4096]{1,0:T(2,128)} %co_hbm.1, s32[2,2048]{1,0:T(2,128)} %sl_hbm.1), custom_call_target="tpu_custom_call" | custom-call | tf_op jit(solution)/shard_map/pallas_call | solution.py:449
  23.3 0.6 %copy.5 = f32[8,128]{1,0:T(8,128)} copy(f32[8,128]{1,0:T(8,128)S(1)} %shard_map.37) | data formatting | bytes 8192

commit v4 on v3

--- a/solution.py
+++ b/solution.py
@@ -45,9 +45,10 @@
 
 def kernel(
     x_hbm, co_hbm, sl_hbm, out_ref,
-    xv, cov, slv, raw_send, raw_recv, side_send, side_recv, part_send, part_recv, tot_send, tot_recv, pow_send, pow_recv,
+    xv, cov, slv, raw_send, raw_recv, more_recv, side_send, side_recv, part_send, part_recv, tot_send, tot_recv, pow_send, pow_recv,
     tabc, tabt, tabr, xrot, wbuf, accum,
-    in_sem, late_sem, go_sem, side_ss, side_rs, part_ss, part_rs, raw_ss, raw_rs, tot_ss, tot_rs, forward_ss, pow_ss, pow_rs,
+    tabc2, tabt2, tabr2, xrot2, wbuf2, accum2,
+    in_sem, late_sem, go_sem, side_ss, side_rs, part_ss, part_rs, raw_ss, more_ss, raw_rs, tot_ss, tot_rs, forward_ss, pow_ss, pow_rs,
 ):
     bi = lax.axis_index("bins")
     sj = lax.axis_index("sta")
@@ -63,6 +64,9 @@
 
     early = pz < 2
     late = pz >= 2
+    first_row = (pz == 0) & (pl_lo == 0)
+    next_row = (pz == 1) & (pl_lo == 0)
+    plain = (pz >= 2) | (pl_lo == 1)
     rows = (pz, pz + 1 - 2 * lax.rem(pz, 2), 3 - pz, lax.rem(pz + 2, 4))
 
     def sta_at(n, dy):
@@ -157,20 +161,33 @@
             device_id=(chip, sj), device_id_type=MESH,
         )
 
+    def more_copy(n, dy):
+        q = sta_at(n, dy)
+        return pltpu.make_async_remote_copy(
+            src_ref=raw_send.at[lax.rem(q, 4) + 4], dst_ref=more_recv.at[sj],
+            send_sem=more_ss, recv_sem=raw_rs.at[n // 2],
+            device_id=(bi, q), device_id_type=MESH,
+        )
+
     def send_raw(n):
         for dy in FAR_Y:
             if (n, dy) != (0, 0):
                 raw_copy(n, dy).start()
 
+        @pl.when((pz == (0, 1, 3, 2)[n]) & (pl_lo == 0))
+        def _():
+            for dy in FAR_Y:
+                if (n, dy) != (0, 0):
+                    more_copy(n, dy).start()
+
     def send_tot(n):
         for dy in FAR_Y:
             if (n, dy) != (0, 0):
                 tot_copy(n, dy).start()
 
-    def pow_copy(d):
-        m = lax.rem(own + d, 8)
+    def pow_copy(tile, m, slot):
         return pltpu.make_async_remote_copy(
-            src_ref=pow_send.at[m], dst_ref=pow_recv.at[own],
+            src_ref=pow_send.at[tile], dst_ref=pow_recv.at[slot],
             send_sem=pow_ss, recv_sem=pow_rs,
             device_id=(bi, pair * 8 + m), device_id_type=MESH,
         )
@@ -233,6 +250,10 @@
 
         raw_recv[sj] = raw_send[own]
 
+        @pl.when(first_row)
+        def _():
+            more_recv[sj] = raw_send[own + 4]
+
     loads[1].wait()
     loads[2].wait()
     row8 = iota((8, 256), 0)
@@ -240,10 +261,10 @@
     coarse = row8 * 8 + 4
     fine = jnp.where(row8 == 0, 1, 3)
 
-    def tables(j):
+    def tables(j, f, tabc, tabt, tabr):
         lanes = pl.ds(pl.multiple_of(j * 256, 256), 256)
-        cx = cov[0:1, lanes] * f1
-        cy = cov[1:2, lanes] * f1
+        cx = cov[0:1, lanes] * f
+        cy = cov[1:2, lanes] * f
         c, s = cos_sin(coarse * cx)
         tabc[0, :, lanes] = c
         tabc[1, :, lanes] = s
@@ -254,12 +275,16 @@
         cols = []
         for trig in range(2):
             for tab in (cyt, syt):
-                for f in range(2):
-                    cols.append(tabr[trig, f : f + 1, lanes] * tab)
+                for k in range(2):
+                    cols.append(tabr[trig, k : k + 1, lanes] * tab)
         tabt[lanes, :] = jnp.concatenate(cols, 0).astype(jnp.bfloat16).T
 
     with scope("f_tables"):
-        loop(0, 16, tables)
+        loop(0, 16, lambda j: tables(j, f1, tabc, tabt, tabr))
+
+        @pl.when(first_row)
+        def _():
+            loop(0, 16, lambda j: tables(j, f1 + 4, tabc2, tabt2, tabr2))
 
     @pl.when(core == 1)
     def _():
@@ -331,7 +356,12 @@
             send_raw(1)
             send_raw(0)
 
-    def rotate(n):
+    first = (raw_recv, tabc, tabt, tabr, xrot, wbuf, accum)
+    second = (more_recv, tabc2, tabt2, tabr2, xrot2, wbuf2, accum2)
+
+    def rotate(n, bufs):
+        raw_recv, tabc, tabt, tabr, xrot, wbuf, accum = bufs
+
         def block(y):
             j = rows[n] * 4 + y
             lanes = pl.ds(pl.multiple_of(j * 256, 256), 256)
@@ -345,49 +375,35 @@
 
         loop(0, 4, block)
 
-    for n in range(4):
-        if n % 2 == 0:
-            with scope("j_rawwait"):
-                wait_all(raw_recv, 7 + n // 2, raw_rs.at[n // 2])
-            with scope("k_rotate"):
-                rotate(n)
-                rotate(n + 1)
-        with scope("l_totwait%d" % n):
-            @pl.when(core == 0)
-            def _(n=n):
-                wait_all(tot_recv, 4, tot_rs.at[n])
-
-            @pl.when(core == 1)
-            def _(n=n):
-                wait_all(tot_recv, 4 if n else 3, tot_rs.at[n])
-                forward_copy(n).start()
-        with scope("m_main"):
-            lanes = pl.ds(pl.multiple_of(rows[n] * 1024, 1024), 1024)
-            at = slice(n * 1024, n * 1024 + 1024)
-            parts = []
-            for y in range(4):
-                total = tot_recv[rows[n] * 4 + y].astype(jnp.float32)
-                parts += [total[:8], total[8:]]
-            inv = lax.rsqrt(jnp.concatenate(parts, 1) * (1.0 / 256) + epsilon)
-            wbuf[0:8, at] = xrot[0:8, lanes] * inv
-            wbuf[8:16, at] = xrot[8:16, lanes] * inv
-            v = []
-            for trig in range(2):
-                tab = tabc[trig, :, lanes]
-                for row in range(16):
-                    v.append(wbuf[row : row + 1, at] * tab)
-            acc = jnp.dot(
-                jnp.concatenate(v, 0).astype(jnp.bfloat16), tabt[lanes, :], preferred_element_type=jnp.float32
-            )
-            if n == 0:
-                accum[...] = acc
-            elif n < 3:
-                accum[...] += acc
-            else:
-                acc = acc + accum[...]
-
-    with scope("n_post"):
-        mark = jnp.where(iota((128, 128), 1) < 64, -1.0, 1.0)
+    def scales(n):
+        parts = []
+        for y in range(4):
+            total = tot_recv[rows[n] * 4 + y].astype(jnp.float32)
+            parts += [total[:8], total[8:]]
+        return lax.rsqrt(jnp.concatenate(parts, 1) * (1.0 / 256) + epsilon)
+
+    def amplitudes(n, inv, bufs):
+        raw_recv, tabc, tabt, tabr, xrot, wbuf, accum = bufs
+        lanes = pl.ds(pl.multiple_of(rows[n] * 1024, 1024), 1024)
+        at = slice(n * 1024, n * 1024 + 1024)
+        wbuf[0:8, at] = xrot[0:8, lanes] * inv
+        wbuf[8:16, at] = xrot[8:16, lanes] * inv
+        v = []
+        for trig in range(2):
+            tab = tabc[trig, :, lanes]
+            for row in range(16):
+                v.append(wbuf[row : row + 1, at] * tab)
+        acc = jnp.dot(
+            jnp.concatenate(v, 0).astype(jnp.bfloat16), tabt[lanes, :], preferred_element_type=jnp.float32
+        )
+        if n == 3:
+            return acc + accum[...]
+        if n == 0:
+            accum[...] = acc
+        else:
+            accum[...] += acc
+
+    def powers(acc):
         cc, cs, sc, ss = acc[:128, :128], acc[:128, 128:], acc[128:, :128], acc[128:, 128:]
         grid = []
 
@@ -405,9 +421,11 @@
             grid.append(seg_sum(plus[:64] + turned) + pltpu.roll(seg_sum(plus[:64] - turned), 64, 1))
             turned = pltpu.roll(minus[64:], 64, 1)
             grid.append(seg_sum(minus[:64] - turned) + pltpu.roll(seg_sum(minus[:64] + turned), 64, 1))
-        grid = jnp.concatenate(grid, 0) * (1.0 / 32768)
+        return jnp.concatenate(grid, 0) * (1.0 / 32768)
+
+    def pick(grid, tiles, base):
         row = iota((8, 128), 0)
-        for n in range(8):
+        for n in range(tiles):
             at = slice(128 * n, 128 * n + 128)
             col = jnp.broadcast_to(pick_col[:, at], (8, 128))
             hit = jnp.broadcast_to(pick_row[:, at], (8, 128))
@@ -415,10 +433,79 @@
             for k in range(4):
                 values = jnp.take_along_axis(grid[8 * k : 8 * k + 8], col, axis=1)
                 total = total + jnp.where(row + 8 * k == hit, values, 0.0)
-            pow_send[n] = jnp.sum(total, 0, keepdims=True)
+            pow_send[base + n] = jnp.sum(total, 0, keepdims=True)
+
+    mark = jnp.where(iota((128, 128), 1) < 64, -1.0, 1.0)
+
+    for n in range(4):
+        if n % 2 == 0:
+            with scope("j_rawwait"):
+                @pl.when(first_row)
+                def _(n=n):
+                    wait_all(raw_recv, 14 + n, raw_rs.at[n // 2])
+
+                @pl.when(next_row | plain)
+                def _(n=n):
+                    wait_all(raw_recv, 7 + n // 2, raw_rs.at[n // 2])
+
+            with scope("k_rotate"):
+                rotate(n, first)
+                rotate(n + 1, first)
+
+                @pl.when(first_row)
+                def _(n=n):
+                    rotate(n, second)
+                    rotate(n + 1, second)
+
+        with scope("l_totwait%d" % n):
+            @pl.when(core == 0)
+            def _(n=n):
+                wait_all(tot_recv, 4, tot_rs.at[n])
+
+            @pl.when(core == 1)
+            def _(n=n):
+                wait_all(tot_recv, 4 if n else 3, tot_rs.at[n])
+                forward_copy(n).start()
+
+        with scope("m_main"):
+            @pl.when(first_row)
+            def _(n=n):
+                inv = scales(n)
+                acc = amplitudes(n, inv, first)
+                acc2 = amplitudes(n, inv, second)
+                if n == 3:
+                    pick(powers(acc2), 4, 8)
+                    pick(powers(acc), 8, 0)
+
+            @pl.when(next_row | plain)
+            def _(n=n):
+                acc = amplitudes(n, scales(n), first)
+                if n == 3:
+                    pick(powers(acc), 8, 0)
+
     with scope("o_powsend"):
-        for d in range(7, 0, -1):
-            pow_copy(d).start()
+        @pl.when(first_row)
+        def _():
+            for dy in (2, 1, 3):
+                m = lax.rem(own + dy, 4)
+                pow_copy(8 + m, m, own + 4).start()
+                pow_copy(m, m, own).start()
+            for y in range(4, 8):
+                pow_copy(y, y, own).start()
+            pow_recv[own + 4] = pow_send[8 + own]
+
+        @pl.when(next_row)
+        def _():
+            for dy in (2, 1, 3):
+                m = 4 + lax.rem(own + dy, 4)
+                pow_copy(m, m, own).start()
+
+        @pl.when(plain)
+        def _():
+            for d in range(7, 0, -1):
+                m = lax.rem(own + d, 8)
+                pow_copy(m, m, own).start()
+
         pow_recv[own] = pow_send[own]
 
     with scope("p_sendwait"):
@@ -434,13 +521,30 @@
 
         wait_all(raw_recv, 15, raw_ss)
 
+        @pl.when(first_row)
+        def _():
+            wait_all(more_recv, 3, more_ss)
+
+        @pl.when((pz > 0) & (pl_lo == 0))
+        def _():
+            wait_all(more_recv, 4, more_ss)
+
     with scope("q_powwait"):
-        wait_all(pow_recv, 7, pow_rs)
+        @pl.when(first_row)
+        def _():
+            wait_all(pow_send, 6, pow_rs)
+
+        @pl.when(next_row | plain)
+        def _():
+            wait_all(pow_send, 7, pow_rs)
 
     with scope("r_end"):
         for b in range(8):
             out_ref[b : b + 1, :] = pow_recv[b]
-        wait_all(pow_recv, 7, pow_ss)
+        for row, count in ((first_row, 10), (next_row, 3), (plain, 7)):
+            @pl.when(row)
+            def _(count=count):
+                wait_all(pow_send, count, pow_ss)
 
 
 def local(spectra, coords, slowness):
@@ -457,14 +561,21 @@
             pltpu.VMEM((2, 2048), i32),
             pltpu.VMEM((8, 32, 128), bf16),
             pltpu.VMEM((16, 32, 128), bf16),
+            pltpu.VMEM((16, 32, 128), bf16),
             pltpu.VMEM((16, 128), f32),
             pltpu.VMEM((16, 128), f32),
             pltpu.VMEM((16, 128), bf16),
             pltpu.VMEM((8, 16, 128), bf16),
             pltpu.VMEM((16, 128), bf16),
             pltpu.VMEM((16, 16, 128), bf16),
+            pltpu.VMEM((12, 1, 128), f32),
             pltpu.VMEM((8, 1, 128), f32),
-            pltpu.VMEM((8, 1, 128), f32),
+            pltpu.VMEM((2, 8, 4096), f32),
+            pltpu.VMEM((4096, 256), bf16),
+            pltpu.VMEM((2, 8, 4096), f32),
+            pltpu.VMEM((16, 4096), f32),
+            pltpu.VMEM((16, 4096), f32),
+            pltpu.VMEM((256, 256), f32),
             pltpu.VMEM((2, 8, 4096), f32),
             pltpu.VMEM((4096, 256), bf16),
             pltpu.VMEM((2, 8, 4096), f32),
@@ -475,7 +586,7 @@
             pltpu.SemaphoreType.REGULAR,
             pltpu.SemaphoreType.REGULAR((2,)),
             dma, dma,
-            dma, dma, dma, dma((2,)), dma, dma((4,)), dma, dma, dma,
+            dma, dma, dma, dma, dma((2,)), dma, dma((4,)), dma, dma, dma,
         ],
         compiler_params=pltpu.CompilerParams(
             collective_id=0, has_side_effects=True, vmem_limit_bytes=56540000

time: 24 us -> 23.3 us (0.971)
  Pallas kernels: 23.3 us -> 22.6 us
    pallas_call x1, Pallas kernels: 23.3 us -> 22.6 us  [local(): pl.pallas_call(kernel, out_shape=jax.ShapeDtypeStruct((8, 128), f32), in_...]
where the time goes in v4:
time: 23.3 us; the launch traced here: 23.2 us
  Pallas kernels  22.6 us (97%)
  local copies, waits for them, and re-layouts  0.6 us (3%)
    pallas_call x1, Pallas kernels, local(): pl.pallas_call(kernel, out_shape=jax.ShapeDtypeStruct((8, 128), f32), in_...  22.6 us
    unnamed x1, local copies, waits for them, and re-layouts  0.6 us

profile of v4, /device:TPU:1, one launch (start us, length us, event | category | flops | bytes accessed | tf_op | source)
XLA Modules:
  0.0 23.2 jit_solution(10559222307509299806)
XLA Ops:
  0.0 22.6 %shard_map.37 = f32[8,128]{1,0:T(8,128)S(1)} custom-call(bf16[2,8,8,256]{3,2,1,0:T(8,128)(2,1)} %x_hbm.1, s32[2,4096]{1,0:T(2,128)} %co_hbm.1, s32[2,2048]{1,0:T(2,128)} %sl_hbm.1), custom_call_target="tpu_custom_call" | custom-call | tf_op jit(solution)/shard_map/pallas_call | solution.py:553
  22.6 0.6 %copy.5 = f32[8,128]{1,0:T(8,128)} copy(f32[8,128]{1,0:T(8,128)S(1)} %shard_map.37) | data formatting | bytes 8192

commit v5 on v4

--- a/solution.py
+++ b/solution.py
@@ -274,7 +274,7 @@
         cyt, syt = cos_sin(odd32 * cy)
         cols = []
         for trig in range(2):
-            for tab in (cyt, syt):
+            for tab in (cyt, -syt):
                 for k in range(2):
                     cols.append(tabr[trig, k : k + 1, lanes] * tab)
         tabt[lanes, :] = jnp.concatenate(cols, 0).astype(jnp.bfloat16).T
@@ -325,8 +325,8 @@
         c01 = jnp.where(cpos, 1, 0)
         rel = jnp.where(c01 == jnp.where(fpos, 1, 0), 0, 1)
         diff = jnp.where(c01 == jnp.where(ypos, 1, 0), 0, 1)
-        pick_row = (rel * 2 + diff) * 8 + cidx
-        pick_col = (1 - c01) * 64 + fidx * 32 + ky
+        pick_row = (rel * 2 + 1 - c01) * 8 + cidx
+        pick_col = diff * 64 + fidx * 32 + ky
     with scope("i_late"):
         @pl.when(early & (core == 1))
         def _():
@@ -396,12 +396,11 @@
         acc = jnp.dot(
             jnp.concatenate(v, 0).astype(jnp.bfloat16), tabt[lanes, :], preferred_element_type=jnp.float32
         )
-        if n == 3:
-            return acc + accum[...]
         if n == 0:
             accum[...] = acc
-        else:
+        elif n == 1:
             accum[...] += acc
+        return acc
 
     def powers(acc):
         cc, cs, sc, ss = acc[:128, :128], acc[:128, 128:], acc[128:, :128], acc[128:, 128:]
@@ -415,12 +414,11 @@
             return total
 
         for x, y in ((cc - ss, sc + cs), (cc + ss, sc - cs)):
-            y = pltpu.roll(y, 64, 1) * mark
+            y = pltpu.roll(y, 64, 1)
             plus, minus = x + y, x - y
-            turned = pltpu.roll(plus[64:], 64, 1)
-            grid.append(seg_sum(plus[:64] + turned) + pltpu.roll(seg_sum(plus[:64] - turned), 64, 1))
-            turned = pltpu.roll(minus[64:], 64, 1)
-            grid.append(seg_sum(minus[:64] - turned) + pltpu.roll(seg_sum(minus[:64] + turned), 64, 1))
+            turn_plus, turn_minus = pltpu.roll(plus[64:], 64, 1), pltpu.roll(minus[64:], 64, 1)
+            grid.append(seg_sum(plus[:64] - turn_minus) + pltpu.roll(seg_sum(minus[:64] + turn_plus), 64, 1))
+            grid.append(seg_sum(plus[:64] + turn_minus) + pltpu.roll(seg_sum(minus[:64] - turn_plus), 64, 1))
         return jnp.concatenate(grid, 0) * (1.0 / 32768)
 
     def pick(grid, tiles, base):
@@ -435,8 +433,6 @@
                 total = total + jnp.where(row + 8 * k == hit, values, 0.0)
             pow_send[base + n] = jnp.sum(total, 0, keepdims=True)
 
-    mark = jnp.where(iota((128, 128), 1) < 64, -1.0, 1.0)
-
     for n in range(4):
         if n % 2 == 0:
             with scope("j_rawwait"):
@@ -457,31 +453,58 @@
                     rotate(n, second)
                     rotate(n + 1, second)
 
-        with scope("l_totwait%d" % n):
+        def take_totals(n):
             @pl.when(core == 0)
-            def _(n=n):
+            def _():
                 wait_all(tot_recv, 4, tot_rs.at[n])
 
             @pl.when(core == 1)
-            def _(n=n):
+            def _():
                 wait_all(tot_recv, 4 if n else 3, tot_rs.at[n])
                 forward_copy(n).start()
 
+        with scope("l_totwait%d" % n):
+            if n == 2:
+                @pl.when(pz == 0)
+                def _():
+                    take_totals(3)
+
+            if n == 3:
+                @pl.when(pz > 0)
+                def _():
+                    take_totals(3)
+            else:
+                take_totals(n)
+
         with scope("m_main"):
-            @pl.when(first_row)
-            def _(n=n):
-                inv = scales(n)
-                acc = amplitudes(n, inv, first)
-                acc2 = amplitudes(n, inv, second)
-                if n == 3:
-                    pick(powers(acc2), 4, 8)
-                    pick(powers(acc), 8, 0)
-
-            @pl.when(next_row | plain)
-            def _(n=n):
-                acc = amplitudes(n, scales(n), first)
-                if n == 3:
-                    pick(powers(acc), 8, 0)
+            if n < 2:
+                @pl.when(first_row)
+                def _(n=n):
+                    inv = scales(n)
+                    amplitudes(n, inv, first)
+                    amplitudes(n, inv, second)
+
+                @pl.when(next_row | plain)
+                def _(n=n):
+                    amplitudes(n, scales(n), first)
+            elif n == 2:
+                @pl.when(first_row)
+                def _():
+                    inv = [scales(2), scales(3)]
+                    pick(powers(amplitudes(2, inv[0], second) + amplitudes(3, inv[1], second) + accum2[...]), 4, 8)
+                    pick(powers(amplitudes(2, inv[0], first) + amplitudes(3, inv[1], first) + accum[...]), 8, 0)
+
+                @pl.when((pz == 0) & (pl_lo == 1))
+                def _():
+                    pick(powers(amplitudes(2, scales(2), first) + amplitudes(3, scales(3), first) + accum[...]), 8, 0)
+
+                @pl.when(pz > 0)
+                def _():
+                    accum[...] += amplitudes(2, scales(2), first)
+            else:
+                @pl.when(pz > 0)
+                def _():
+                    pick(powers(amplitudes(3, scales(3), first) + accum[...]), 8, 0)
 
     with scope("o_powsend"):
         @pl.when(first_row)

time: 23.3 us -> 23.1 us (level)
  no operation moved by 1% of the time
where the time goes in v5:
time: 23.1 us; the launch traced here: 23 us
  Pallas kernels  22.4 us (97%)
  local copies, waits for them, and re-layouts  0.6 us (3%)
    pallas_call x1, Pallas kernels, local(): pl.pallas_call(kernel, out_shape=jax.ShapeDtypeStruct((8, 128), f32), in_...  22.4 us
    unnamed x1, local copies, waits for them, and re-layouts  0.6 us

profile of v5, /device:TPU:1, one launch (start us, length us, event | category | flops | bytes accessed | tf_op | source)
XLA Modules:
  0.0 23.0 jit_solution(11800076419579027408)
XLA Ops:
  0.0 22.4 %shard_map.37 = f32[8,128]{1,0:T(8,128)S(1)} custom-call(bf16[2,8,8,256]{3,2,1,0:T(8,128)(2,1)} %x_hbm.1, s32[2,4096]{1,0:T(2,128)} %co_hbm.1, s32[2,2048]{1,0:T(2,128)} %sl_hbm.1), custom_call_target="tpu_custom_call" | custom-call | tf_op jit(solution)/shard_map/pallas_call | solution.py:576
  22.4 0.6 %copy.5 = f32[8,128]{1,0:T(8,128)} copy(f32[8,128]{1,0:T(8,128)S(1)} %shard_map.37) | data formatting | bytes 8192

commit v6 on v4

--- a/solution.py
+++ b/solution.py
@@ -274,7 +274,7 @@
         cyt, syt = cos_sin(odd32 * cy)
         cols = []
         for trig in range(2):
-            for tab in (cyt, syt):
+            for tab in (cyt, -syt):
                 for k in range(2):
                     cols.append(tabr[trig, k : k + 1, lanes] * tab)
         tabt[lanes, :] = jnp.concatenate(cols, 0).astype(jnp.bfloat16).T
@@ -325,8 +325,8 @@
         c01 = jnp.where(cpos, 1, 0)
         rel = jnp.where(c01 == jnp.where(fpos, 1, 0), 0, 1)
         diff = jnp.where(c01 == jnp.where(ypos, 1, 0), 0, 1)
-        pick_row = (rel * 2 + diff) * 8 + cidx
-        pick_col = (1 - c01) * 64 + fidx * 32 + ky
+        pick_row = (rel * 2 + 1 - c01) * 8 + cidx
+        pick_col = diff * 64 + fidx * 32 + ky
     with scope("i_late"):
         @pl.when(early & (core == 1))
         def _():
@@ -396,12 +396,7 @@
         acc = jnp.dot(
             jnp.concatenate(v, 0).astype(jnp.bfloat16), tabt[lanes, :], preferred_element_type=jnp.float32
         )
-        if n == 3:
-            return acc + accum[...]
-        if n == 0:
-            accum[...] = acc
-        else:
-            accum[...] += acc
+        return acc if n == 0 else acc + accum[...]
 
     def powers(acc):
         cc, cs, sc, ss = acc[:128, :128], acc[:128, 128:], acc[128:, :128], acc[128:, 128:]
@@ -415,12 +410,11 @@
             return total
 
         for x, y in ((cc - ss, sc + cs), (cc + ss, sc - cs)):
-            y = pltpu.roll(y, 64, 1) * mark
+            y = pltpu.roll(y, 64, 1)
             plus, minus = x + y, x - y
-            turned = pltpu.roll(plus[64:], 64, 1)
-            grid.append(seg_sum(plus[:64] + turned) + pltpu.roll(seg_sum(plus[:64] - turned), 64, 1))
-            turned = pltpu.roll(minus[64:], 64, 1)
-            grid.append(seg_sum(minus[:64] - turned) + pltpu.roll(seg_sum(minus[:64] + turned), 64, 1))
+            turn_plus, turn_minus = pltpu.roll(plus[64:], 64, 1), pltpu.roll(minus[64:], 64, 1)
+            grid.append(seg_sum(plus[:64] - turn_minus) + pltpu.roll(seg_sum(minus[:64] + turn_plus), 64, 1))
+            grid.append(seg_sum(plus[:64] + turn_minus) + pltpu.roll(seg_sum(minus[:64] - turn_plus), 64, 1))
         return jnp.concatenate(grid, 0) * (1.0 / 32768)
 
     def pick(grid, tiles, base):
@@ -435,8 +429,6 @@
                 total = total + jnp.where(row + 8 * k == hit, values, 0.0)
             pow_send[base + n] = jnp.sum(total, 0, keepdims=True)
 
-    mark = jnp.where(iota((128, 128), 1) < 64, -1.0, 1.0)
-
     for n in range(4):
         if n % 2 == 0:
             with scope("j_rawwait"):
@@ -457,31 +449,51 @@
                     rotate(n, second)
                     rotate(n + 1, second)
 
-        with scope("l_totwait%d" % n):
+        def take_totals(n):
             @pl.when(core == 0)
-            def _(n=n):
+            def _():
                 wait_all(tot_recv, 4, tot_rs.at[n])
 
             @pl.when(core == 1)
-            def _(n=n):
+            def _():
                 wait_all(tot_recv, 4 if n else 3, tot_rs.at[n])
                 forward_copy(n).start()
 
+        with scope("l_totwait%d" % n):
+            if n < 2:
+                take_totals(n)
+            else:
+                @pl.when(pz == 0)
+                def _(n=n):
+                    take_totals(5 - n)
+
+                @pl.when(pz > 0)
+                def _(n=n):
+                    take_totals(n)
+
         with scope("m_main"):
+            at_row0 = 5 - n if n > 1 else n
+
             @pl.when(first_row)
             def _(n=n):
-                inv = scales(n)
-                acc = amplitudes(n, inv, first)
-                acc2 = amplitudes(n, inv, second)
+                inv = scales(at_row0)
+                acc2 = amplitudes(at_row0, inv, second)
+                acc = amplitudes(at_row0, inv, first)
                 if n == 3:
                     pick(powers(acc2), 4, 8)
                     pick(powers(acc), 8, 0)
-
-            @pl.when(next_row | plain)
-            def _(n=n):
-                acc = amplitudes(n, scales(n), first)
-                if n == 3:
-                    pick(powers(acc), 8, 0)
+                else:
+                    accum2[...] = acc2
+                    accum[...] = acc
+
+            for row, k in ((pz == 0) & (pl_lo == 1), at_row0), (pz > 0, n):
+                @pl.when(row)
+                def _(n=n, k=k):
+                    acc = amplitudes(k, scales(k), first)
+                    if n == 3:
+                        pick(powers(acc), 8, 0)
+                    else:
+                        accum[...] = acc
 
     with scope("o_powsend"):
         @pl.when(first_row)

time: 23.3 us -> 23 us (0.987)
  Pallas kernels: 22.6 us -> 22.3 us
    pallas_call x1, Pallas kernels: 22.6 us -> 22.3 us  [local(): pl.pallas_call(kernel, out_shape=jax.ShapeDtypeStruct((8, 128), f32), in_...]
where the time goes in v6:
time: 23 us; the launch traced here: 22.9 us
  Pallas kernels  22.3 us (97%)
  local copies, waits for them, and re-layouts  0.6 us (3%)
    pallas_call x1, Pallas kernels, local(): pl.pallas_call(kernel, out_shape=jax.ShapeDtypeStruct((8, 128), f32), in_...  22.3 us
    unnamed x1, local copies, waits for them, and re-layouts  0.6 us

profile of v6, /device:TPU:1, one launch (start us, length us, event | category | flops | bytes accessed | tf_op | source)
XLA Modules:
  0.0 22.9 jit_solution(1983798385137373040)
XLA Ops:
  0.0 22.3 %shard_map.37 = f32[8,128]{1,0:T(8,128)S(1)} custom-call(bf16[2,8,8,256]{3,2,1,0:T(8,128)(2,1)} %x_hbm.1, s32[2,4096]{1,0:T(2,128)} %co_hbm.1, s32[2,2048]{1,0:T(2,128)} %sl_hbm.1), custom_call_target="tpu_custom_call" | custom-call | tf_op jit(solution)/shard_map/pallas_call | solution.py:565
  22.3 0.6 %copy.5 = f32[8,128]{1,0:T(8,128)} copy(f32[8,128]{1,0:T(8,128)S(1)} %shard_map.37) | data formatting | bytes 8192

commit v7 on v6

--- a/solution.py
+++ b/solution.py
@@ -48,7 +48,7 @@
     xv, cov, slv, raw_send, raw_recv, more_recv, side_send, side_recv, part_send, part_recv, tot_send, tot_recv, pow_send, pow_recv,
     tabc, tabt, tabr, xrot, wbuf, accum,
     tabc2, tabt2, tabr2, xrot2, wbuf2, accum2,
-    in_sem, late_sem, go_sem, side_ss, side_rs, part_ss, part_rs, raw_ss, more_ss, raw_rs, tot_ss, tot_rs, forward_ss, pow_ss, pow_rs,
+    in_sem, late_sem, go_sem, side_rs, part_rs, raw_rs, tot_rs, pow_rs, sent, pow_ss,
 ):
     bi = lax.axis_index("bins")
     sj = lax.axis_index("sta")
@@ -77,7 +77,7 @@
 
     loads = [
         pltpu.make_async_copy(src, dst, in_sem.at[n])
-        for n, (src, dst) in enumerate(((x_hbm, xv), (co_hbm, cov), (sl_hbm, slv)))
+        for n, src, dst in ((0, x_hbm, xv), (1, co_hbm, cov), (1, sl_hbm, slv))
     ]
     for load in loads:
         load.start()
@@ -125,7 +125,7 @@
         side_send[...] = side
 
     side_copy = pltpu.make_async_remote_copy(
-        src_ref=side_send, dst_ref=side_recv, send_sem=side_ss, recv_sem=side_rs,
+        src_ref=side_send, dst_ref=side_recv, send_sem=sent, recv_sem=side_rs,
         device_id=(chip + 1, sj), device_id_type=MESH,
     )
 
@@ -135,7 +135,7 @@
     def part_copy(n):
         return pltpu.make_async_remote_copy(
             src_ref=part_send, dst_ref=part_recv.at[lax.div(bi, 2)],
-            send_sem=part_ss, recv_sem=part_rs,
+            send_sem=sent, recv_sem=part_rs,
             device_id=(chip_at(FAR_BINS[n]) + 1, sj), device_id_type=MESH,
         )
 
@@ -143,21 +143,21 @@
         q = sta_at(n, dy)
         return pltpu.make_async_remote_copy(
             src_ref=raw_send.at[lax.rem(q, 8)], dst_ref=raw_recv.at[sj],
-            send_sem=raw_ss, recv_sem=raw_rs.at[n // 2],
+            send_sem=sent, recv_sem=raw_rs.at[n // 2],
             device_id=(bi, q), device_id_type=MESH,
         )
 
     def tot_copy(n, dy):
         return pltpu.make_async_remote_copy(
             src_ref=tot_send, dst_ref=tot_recv.at[sj],
-            send_sem=tot_ss, recv_sem=tot_rs.at[n],
+            send_sem=sent, recv_sem=tot_rs.at[n],
             device_id=(bi, sta_at(n, dy)), device_id_type=MESH,
         )
 
     def forward_copy(n):
         block = tot_recv.at[pl.ds(rows[n] * 4, 4)]
         return pltpu.make_async_remote_copy(
-            src_ref=block, dst_ref=block, send_sem=forward_ss, recv_sem=tot_rs.at[n],
+            src_ref=block, dst_ref=block, send_sem=sent, recv_sem=tot_rs.at[n],
             device_id=(chip, sj), device_id_type=MESH,
         )
 
@@ -165,7 +165,7 @@
         q = sta_at(n, dy)
         return pltpu.make_async_remote_copy(
             src_ref=raw_send.at[lax.rem(q, 4) + 4], dst_ref=more_recv.at[sj],
-            send_sem=more_ss, recv_sem=raw_rs.at[n // 2],
+            send_sem=sent, recv_sem=raw_rs.at[n // 2],
             device_id=(bi, q), device_id_type=MESH,
         )
 
@@ -238,11 +238,16 @@
             pl.semaphore_wait(go_sem.at[0], 1)
 
     with scope("e_send1"):
-        @pl.when(late)
+        @pl.when(pz == 2)
         def _():
             send_raw(3)
             send_raw(2)
 
+        @pl.when(pz == 3)
+        def _():
+            send_raw(2)
+            send_raw(3)
+
         @pl.when(early)
         def _():
             send_raw(1)
@@ -254,8 +259,7 @@
         def _():
             more_recv[sj] = raw_send[own + 4]
 
-    loads[1].wait()
-    loads[2].wait()
+    wait_all(tabt, 96, in_sem.at[1])
     row8 = iota((8, 256), 0)
     odd32 = iota((32, 256), 0) * 2 + 1
     coarse = row8 * 8 + 4
@@ -297,10 +301,15 @@
             total = total.astype(jnp.bfloat16)
             tot_send[...] = total
 
-            @pl.when(late)
+            @pl.when(pz == 2)
             def _():
                 send_tot(3)
                 send_tot(2)
+
+            @pl.when(pz == 3)
+            def _():
+                send_tot(2)
+                send_tot(3)
 
             @pl.when(early)
             def _():
@@ -382,7 +391,7 @@
             parts += [total[:8], total[8:]]
         return lax.rsqrt(jnp.concatenate(parts, 1) * (1.0 / 256) + epsilon)
 
-    def amplitudes(n, inv, bufs):
+    def amplitudes(n, inv, bufs, onto=True):
         raw_recv, tabc, tabt, tabr, xrot, wbuf, accum = bufs
         lanes = pl.ds(pl.multiple_of(rows[n] * 1024, 1024), 1024)
         at = slice(n * 1024, n * 1024 + 1024)
@@ -396,7 +405,7 @@
         acc = jnp.dot(
             jnp.concatenate(v, 0).astype(jnp.bfloat16), tabt[lanes, :], preferred_element_type=jnp.float32
         )
-        return acc if n == 0 else acc + accum[...]
+        return acc + accum[...] if n and onto else acc
 
     def powers(acc):
         cc, cs, sc, ss = acc[:128, :128], acc[:128, 128:], acc[128:, :128], acc[128:, 128:]
@@ -417,9 +426,9 @@
             grid.append(seg_sum(plus[:64] + turn_minus) + pltpu.roll(seg_sum(minus[:64] - turn_plus), 64, 1))
         return jnp.concatenate(grid, 0) * (1.0 / 32768)
 
-    def pick(grid, tiles, base):
+    def pick(grid, first_tile, last_tile, base):
         row = iota((8, 128), 0)
-        for n in range(tiles):
+        for n in range(first_tile, last_tile):
             at = slice(128 * n, 128 * n + 128)
             col = jnp.broadcast_to(pick_col[:, at], (8, 128))
             hit = jnp.broadcast_to(pick_row[:, at], (8, 128))
@@ -463,83 +472,83 @@
             if n < 2:
                 take_totals(n)
             else:
-                @pl.when(pz == 0)
-                def _(n=n):
-                    take_totals(5 - n)
+                if n == 3:
+                    @pl.when(pz == 0)
+                    def _():
+                        take_totals(3)
+                        take_totals(2)
 
                 @pl.when(pz > 0)
                 def _(n=n):
                     take_totals(n)
 
         with scope("m_main"):
-            at_row0 = 5 - n if n > 1 else n
-
             @pl.when(first_row)
             def _(n=n):
-                inv = scales(at_row0)
-                acc2 = amplitudes(at_row0, inv, second)
-                acc = amplitudes(at_row0, inv, first)
-                if n == 3:
-                    pick(powers(acc2), 4, 8)
-                    pick(powers(acc), 8, 0)
-                else:
+                if n == 2:
+                    return
+                inv = scales(n)
+                acc2 = amplitudes(n, inv, second)
+                acc = amplitudes(n, inv, first)
+                if n < 2:
                     accum2[...] = acc2
                     accum[...] = acc
-
-            for row, k in ((pz == 0) & (pl_lo == 1), at_row0), (pz > 0, n):
-                @pl.when(row)
-                def _(n=n, k=k):
-                    acc = amplitudes(k, scales(k), first)
-                    if n == 3:
-                        pick(powers(acc), 8, 0)
-                    else:
-                        accum[...] = acc
+                    return
+                inv = scales(2)
+                acc2 = acc2 + amplitudes(2, inv, second, False)
+                acc = acc + amplitudes(2, inv, first, False)
+                pick(powers(acc2), 0, 4, 8)
+                grid = powers(acc)
+                pick(grid, 0, 4, 0)
+                for dy in (2, 1, 3):
+                    m = lax.rem(own + dy, 4)
+                    pow_copy(8 + m, m, own + 4).start()
+                    pow_copy(m, m, own).start()
+                pick(grid, 4, 8, 0)
+                for y in range(4, 8):
+                    pow_copy(y, y, own).start()
+                pow_recv[own + 4] = pow_send[8 + own]
+
+            @pl.when((pz == 0) & (pl_lo == 1))
+            def _(n=n):
+                if n == 2:
+                    return
+                acc = amplitudes(n, scales(n), first)
+                if n < 2:
+                    accum[...] = acc
+                    return
+                acc = acc + amplitudes(2, scales(2), first, False)
+                grid = powers(acc)
+                pick(grid, 0, 4, 0)
+                for dy in (2, 1, 3):
+                    m = lax.rem(own + dy, 4)
+                    pow_copy(m, m, own).start()
+                pick(grid, 4, 8, 0)
+                for y in range(4, 8):
+                    pow_copy(y, y, own).start()
+
+            @pl.when(pz > 0)
+            def _(n=n):
+                acc = amplitudes(n, scales(n), first)
+                if n < 3:
+                    accum[...] = acc
+                    return
+                pick(powers(acc), 0, 8, 0)
 
     with scope("o_powsend"):
-        @pl.when(first_row)
-        def _():
-            for dy in (2, 1, 3):
-                m = lax.rem(own + dy, 4)
-                pow_copy(8 + m, m, own + 4).start()
-                pow_copy(m, m, own).start()
-            for y in range(4, 8):
-                pow_copy(y, y, own).start()
-            pow_recv[own + 4] = pow_send[8 + own]
-
         @pl.when(next_row)
         def _():
             for dy in (2, 1, 3):
                 m = 4 + lax.rem(own + dy, 4)
                 pow_copy(m, m, own).start()
 
-        @pl.when(plain)
-        def _():
-            for d in range(7, 0, -1):
+        @pl.when(plain & (pz > 0))
+        def _():
+            for d in (4, 6, 2, 5, 3, 7, 1):
                 m = lax.rem(own + d, 8)
                 pow_copy(m, m, own).start()
 
         pow_recv[own] = pow_send[own]
-
-    with scope("p_sendwait"):
-        @pl.when(core == 0)
-        def _():
-            side_copy.wait_send()
-
-        @pl.when(core == 1)
-        def _():
-            wait_all(part_recv, 7, part_ss)
-            wait_all(tot_recv, 15, tot_ss)
-            wait_all(tot_recv, 16, forward_ss)
-
-        wait_all(raw_recv, 15, raw_ss)
-
-        @pl.when(first_row)
-        def _():
-            wait_all(more_recv, 3, more_ss)
-
-        @pl.when((pz > 0) & (pl_lo == 0))
-        def _():
-            wait_all(more_recv, 4, more_ss)
 
     with scope("q_powwait"):
         @pl.when(first_row)
@@ -557,6 +566,15 @@
             @pl.when(row)
             def _(count=count):
                 wait_all(pow_send, count, pow_ss)
+
+        for row, count in ((first_row, 6), ((pz > 0) & (pl_lo == 0), 8), (pl_lo == 1, 0)):
+            @pl.when(row & (core == 1))
+            def _(count=count):
+                wait_all(tabt, 8 * (68 + count), sent)
+
+            @pl.when(row & (core == 0))
+            def _(count=count):
+                wait_all(tabt, 8 * (32 + count), sent)
 
 
 def local(spectra, coords, slowness):
@@ -594,11 +612,10 @@
             pltpu.VMEM((16, 4096), f32),
             pltpu.VMEM((16, 4096), f32),
             pltpu.VMEM((256, 256), f32),
-            dma((3,)),
+            dma((2,)),
             pltpu.SemaphoreType.REGULAR,
             pltpu.SemaphoreType.REGULAR((2,)),
-            dma, dma,
-            dma, dma, dma, dma, dma((2,)), dma, dma((4,)), dma, dma, dma,
+            dma, dma, dma((2,)), dma((4,)), dma, dma, dma,
         ],
         compiler_params=pltpu.CompilerParams(
             collective_id=0, has_side_effects=True, vmem_limit_bytes=56540000

time: 23 us -> 22.8 us (level)
  Pallas kernels: 22.3 us -> 22 us
    pallas_call x1, Pallas kernels: 22.3 us -> 22 us  [local(): pl.pallas_call(kernel, out_shape=jax.ShapeDtypeStruct((8, 128), f32), in_...]
where the time goes in v7:
time: 22.8 us; the launch traced here: 22.6 us
  Pallas kernels  22 us (96%)
  local copies, waits for them, and re-layouts  0.6 us (3%)
    pallas_call x1, Pallas kernels, local(): pl.pallas_call(kernel, out_shape=jax.ShapeDtypeStruct((8, 128), f32), in_...  22 us
    unnamed x1, local copies, waits for them, and re-layouts  0.6 us

profile of v7, /device:TPU:1, one launch (start us, length us, event | category | flops | bytes accessed | tf_op | source)
XLA Modules:
  0.0 22.6 jit_solution(15943458245599578384)
XLA Ops:
  0.0 22.0 %shard_map.37 = f32[8,128]{1,0:T(8,128)S(1)} custom-call(bf16[2,8,8,256]{3,2,1,0:T(8,128)(2,1)} %x_hbm.1, s32[2,4096]{1,0:T(2,128)} %co_hbm.1, s32[2,2048]{1,0:T(2,128)} %sl_hbm.1), custom_call_target="tpu_custom_call" | custom-call | tf_op jit(solution)/shard_map/pallas_call | solution.py:583
  22.1 0.6 %copy.5 = f32[8,128]{1,0:T(8,128)} copy(f32[8,128]{1,0:T(8,128)S(1)} %shard_map.37) | data formatting | bytes 8192
